TPU v7x, 32 devices: a whole 2x2x4 slice. The times are simulated.
32 devices in a mesh: wa: 8 (over z, y), ba: 4 (over x, core).
Axes of the slice: x: 2, y: 2, z: 4, core: 2. Of those that a mesh axis runs over, the one named last changes fastest.
Arguments:
- latent: float32 [16, 8, 1024], P('ba', None, 'wa'), parts along dimension 0, may hold values from -12 to 12
- noise: float32 [2, 16, 8, 1024], P(None, 'ba', None, 'wa'), parts along dimension 1, may hold values from -6 to 6
- offsets: int32 [16], P('wa'), may hold values from 0 to 63
- anchors: int32 [2], replicated, may hold values from 0 to 15
- guidance: float32 [1], replicated, may hold values from 0.4 to 0.8
- w_in: bfloat16 [320, 36], replicated, may hold values from -1 to 1
- w_mid: bfloat16 [320, 320], replicated, may hold values from -0.3125 to 0.3125
- w_out: bfloat16 [36, 320], replicated, may hold values from -0.109375 to 0.109375
- t_embed: float32 [2, 320], replicated, may hold values from -6 to 6
- w_feat: float32 [64, 4], replicated, may hold values from -3 to 3
Outputs:
- denoised: float32 [16, 8, 1024], P('ba', None, 'wa'), parts along dimension 0
There are 4 independent parts, one for each index of `ba`. A program takes and returns all parts, laid end to end along the dimension named above; an argument that names none is the same for every part. Nothing has to cross between parts.
All inputs are finite; a program needn't handle non-finite values.
Results may differ from a plain program's by a relative error of at most 0.0065.
Values sent between devices are 32-bit elements; how exact they have to be, the bound alone decides.
A program may use at most 64 MiB of HBM per device.

v0:
```python
import math

import jax
import jax.numpy as jnp
from jax import lax
from jax.sharding import PartitionSpec as P

WIN = 128
STRIDE = 64
STEPS = 2


TAP_SHIFTS = ((-1, -1), (-1, 0), (-1, 1), (0, -1), (0, 0), (0, 1), (1, -1), (1, 0), (1, 1))
CUMULATIVE_ALPHA = (0.35, 0.55, 0.72, 0.85, 0.93)
STABILITY = 1e-06


def spread_2(block, axis, holder):
    block = jnp.where(lax.axis_index(axis) == holder, block, jnp.zeros_like(block))
    return lax.psum(block, axis)


def passed_along(shard, axis, by):
    length = lax.axis_size(axis)
    return lax.ppermute(shard, axis, [(i, (i + by) % length) for i in range(length)])


def plan(number):
    current = CUMULATIVE_ALPHA[number]
    following = CUMULATIVE_ALPHA[number + 1]
    spread = 0.3 * math.sqrt(1.0 - following)
    return (
        math.sqrt(current),
        math.sqrt(1.0 - current),
        math.sqrt(following),
        math.sqrt(1.0 - following - spread * spread),
        spread,
    )


def tapped(field):
    height, columns = (field.shape[-2], field.shape[-1])
    padding = [(0, 0)] * (field.ndim - 2) + [(1, 1), (1, 1)]
    padded = jnp.pad(field, padding)
    return jnp.stack(
        [
            padded[..., 1 + down_by : 1 + down_by + height, 1 + right_by : 1 + right_by + columns]
            for down_by, right_by in TAP_SHIFTS
        ]
    )


def denoise(window, w_in, w_mid, w_out, embedding):
    channels, height, columns = window.shape
    stacked = tapped(window.astype(jnp.bfloat16)).reshape(9 * channels, height * columns)
    hidden_in = jnp.dot(w_in, stacked, preferred_element_type=jnp.float32) + embedding[:, None]
    activated = jax.nn.silu(hidden_in).astype(jnp.bfloat16)
    middle = jnp.dot(w_mid, activated, preferred_element_type=jnp.float32)
    joined = (hidden_in + jax.nn.silu(middle)).astype(jnp.bfloat16)
    outward = jnp.dot(w_out, joined, preferred_element_type=jnp.float32).reshape(
        9, channels, height, columns
    )
    padded = jnp.pad(outward, ((0, 0), (0, 0), (1, 1), (1, 1)))
    result = jnp.zeros((channels, height, columns), jnp.float32)
    for index, (down_by, right_by) in enumerate(TAP_SHIFTS):
        result = (
            result
            + padded[
                index, :, 1 + down_by : 1 + down_by + height, 1 + right_by : 1 + right_by + columns
            ]
        )
    return result


def clean_of(windows, w_in, w_mid, w_out, embedding, now_a, now_s):
    predicted = jax.vmap(denoise, (0, None, None, None, None))(
        windows, w_in, w_mid, w_out, embedding
    )
    cleaned = (windows - now_s * predicted) / now_a
    return (cleaned, predicted)


def percept(cleaned, w_feat):
    return jax.nn.silu(jnp.einsum("fc,chw->fhw", w_feat, cleaned, precision=lax.Precision.HIGHEST))


def mismatch(cleaned, anchor_percept, w_feat):
    difference = percept(cleaned, w_feat) - anchor_percept
    return 0.5 * jnp.sum(difference * difference) / w_feat.shape[0]


def finish_gradient(cleaned, pullback, anchor_percept, w_feat):
    clean_grad = jax.vmap(jax.grad(mismatch), (0, None, None))(cleaned, anchor_percept, w_feat)
    return pullback(clean_grad)[0]


def advance(windows, gradient, predicted, scale, now_a, now_s, next_a, direction):
    return next_a * (windows - scale * gradient - now_s * predicted) / now_a + direction * predicted


def window_update(extended, number, starts, anchors, guidance, w_in, w_mid, w_out, t_embed, w_feat):
    per_dev = starts.shape[0]
    now_a, now_s, next_a, direction, spread = plan(number)
    embedding = t_embed[number]
    windows = jnp.stack(
        [lax.dynamic_slice_in_dim(extended, starts[index], WIN, 2) for index in range(per_dev)]
    )

    def cleaning(inputs):
        return clean_of(inputs, w_in, w_mid, w_out, embedding, now_a, now_s)

    cleaned, pullback, predicted = jax.vjp(cleaning, windows, has_aux=True)
    owner = anchors[number] // per_dev
    slot = anchors[number] % per_dev
    picked = lax.dynamic_index_in_dim(cleaned, slot, 0, keepdims=False)
    anchor_percept = percept(spread_2(picked, "wa", owner), w_feat)
    gradient = finish_gradient(cleaned, pullback, anchor_percept, w_feat)
    square_sum = lax.psum(jnp.sum(gradient * gradient), "wa")
    element_count = per_dev * lax.axis_size("wa") * windows.shape[1] * windows.shape[2] * WIN
    scale = guidance[0] * lax.rsqrt(square_sum / element_count + STABILITY)
    advanced = advance(windows, gradient, predicted, scale, now_a, now_s, next_a, direction)
    summed = jnp.zeros(extended.shape, jnp.float32)
    for index in range(per_dev):
        current = lax.dynamic_slice_in_dim(summed, starts[index], WIN, 2)
        summed = lax.dynamic_update_slice_in_dim(
            summed, current + advanced[index], starts[index], 2
        )
    return (summed, spread)


def local(latent, noise, offsets, anchors, guidance, w_in, w_mid, w_out, t_embed, w_feat):
    width = latent.shape[-1]
    per_dev = offsets.shape[0]
    starts = jnp.arange(per_dev, dtype=jnp.int32) * STRIDE + offsets
    positions = jnp.arange(2 * width, dtype=jnp.int32)
    inside = (positions[None, :] >= starts[:, None]) & (positions[None, :] < starts[:, None] + WIN)
    cover = jnp.sum(inside.astype(jnp.float32), axis=0)
    count_own = cover[:width] + passed_along(cover[width:], "wa", 1)
    state = latent
    for number in range(STEPS):
        neighbour = passed_along(state, "wa", -1)
        extended = jnp.concatenate([state, neighbour], axis=2)
        summed, spread = window_update(
            extended, number, starts, anchors, guidance, w_in, w_mid, w_out, t_embed, w_feat
        )
        spill = passed_along(summed[:, :, width:], "wa", 1)
        state = (summed[:, :, :width] + spill) / count_own + spread * noise[number]
    return state


def solution(mesh):
    return jax.shard_map(
        local,
        mesh=mesh,
        in_specs=(
            P("ba", None, "wa"),
            P(None, "ba", None, "wa"),
            P("wa"),
            P(),
            P(),
            P(),
            P(),
            P(),
            P(),
            P(),
        ),
        out_specs=P("ba", None, "wa"),
        check_vma=False,
    )
```

profile of v0, /device:TPU:0, one launch (start us, length us, event | category | flops | bytes accessed | tf_op | source)
XLA Modules:
  0.0 189.1 jit_solution(8490640891394797083)
XLA Ops:
  0.0 0.8 fusion.239
  0.8 6.0 %collective-permute-start = (f32[4,8,128]{2,0,1:T(4,128)S(1)}, f32[4,8,128]{2,0,1:T(4,128)S(1)}, u32[]{:S(2)}, u32[]{:S(2)}) collective-permute-start(f32[4,8,128]{2,0,1:T(4,128)S(1)} %get-tuple-element.43), channel_id=1, source_target_pairs={{0,28},{4,0},{8,4},{12,8},{16,12},{20,16},{24,20},{28,24},{1,29},{... | collective-permute-start | bytes 49160 | tf_op jit(solution)/shard_map/ppermute | solution.py:25
  8.7 1.4 slice_reduce_fusion
  10.0 1.3 slice_multiply_fusion.1
  11.4 1.3 fusion.240
  20.7 1.3 fusion.190
  22.0 2.6 %fusion.88 = f32[2,1024,320]{1,2,0:T(8,128)} fusion(f32[2,1024,320]{1,2,0:T(8,128)S(1)} %fusion.190, f32[320]{0:T(512)S(1)} %get-tuple-element.6, bf16[320,320]{1,0:T(8,128)(2,1)S(1)} %copy-done), kind=kOutput, calls=%fused_computation.107 | convolution fusion | flops 423362560 | bytes 5448960 | tf_op jit(solution)/shard_map/jvp(vmap())/dot_general | solution.py:58
  24.6 2.7 %fusion.94 = f32[2,36,1024]{2,1,0:T(8,128)S(1)} fusion(f32[2,1024,320]{1,2,0:T(8,128)} %fusion.88, f32[2,1024,320]{1,2,0:T(8,128)S(1)} %fusion.190, f32[320]{0:T(512)S(1)} %get-tuple-element.6, bf16[36,320]{1,0:T(8,128)(2,1)S(1)} %copy-done.2), kind=kOutput, calls=%fused_computation.112 | convolution fusion | flops 51773440 | bytes 5562112 | tf_op jit(solution)/shard_map/jvp(vmap())/dot_general | solution.py:60
  28.2 37.6 %psum.28 = f32[4,8,128]{2,0,1:T(4,128)S(1)} all-reduce(f32[4,8,128]{2,0,1:T(4,128)S(1)} %select_bitcast_fusion.1), channel_id=1, replica_groups=mesh['wa'=8,'ba'=4] {'wa'}, use_global_device_ids=true, to_apply=%region_0.0 | all-reduce | flops 4096 | bytes 32768 | tf_op jit(solution)/shard_map/psum | solution.py:20
  66.2 1.3 fusion.121
  68.1 1.6 convolution_convert_fusion.1
  69.8 5.1 %fusion.110 = bf16[2,36,1024]{2,1,0:T(8,128)(2,1)S(1)} fusion(bf16[2,1024,320]{1,2,0:T(8,128)(2,1)} %convolution_convert_fusion.1, f32[2,1024,320]{1,2,0:T(8,128)S(1)} %fusion.190, f32[2,1024,320]{1,2,0:T(8,128)} %fusion.88, f32[320]{0:T(512)S(1)} %copy-done.14, bf16[320,320]{1,0:T(8,128)(2,1)S(1)} %copy-done, bf16[320,36]{0,1:T(8,128)(2,1)S(1)} %copy-done.1), kind=kOutput, calls=%fused_computation.118 | convolution fusion | flops 482418688 | bytes 6930176 | tf_op jit(solution)/shard_map/transpose(jvp(vmap()))/dot_general | solution.py:56
  75.9 17.8 %psum.29 = f32[]{:T(128)} all-reduce(f32[]{:T(128)} %get-tuple-element.11), channel_id=1, replica_groups=mesh['wa'=8,'ba'=4] {'wa'}, use_global_device_ids=true, to_apply=%region_2.3 | all-reduce | flops 1 | bytes 8 | tf_op jit(solution)/shard_map/psum | solution.py:118
  94.4 1.3 dynamic_update_slice.12
  95.8 1.3 dynamic_update_slice.13
  97.2 2.1 %collective-permute-start.1 = (f32[4,8,128]{2,0,1:T(4,128)S(1)}, f32[4,8,128]{2,0,1:T(4,128)S(1)}, u32[]{:S(2)}, u32[]{:S(2)}) collective-permute-start(f32[4,8,128]{2,0,1:T(4,128)S(1)} %slice.230), channel_id=1, source_target_pairs={{0,4},{4,8},{8,12},{12,16},{16,20},{20,24},{24,28},{28,0},{1,5},{5... | collective-permute-start | bytes 49160 | tf_op jit(solution)/shard_map/ppermute | solution.py:25
  99.9 3.8 %collective-permute-done.1 = f32[4,8,128]{2,0,1:T(4,128)S(1)} collective-permute-done((f32[4,8,128]{2,0,1:T(4,128)S(1)}, f32[4,8,128]{2,0,1:T(4,128)S(1)}, u32[]{:S(2)}, u32[]{:S(2)}) %collective-permute-start.1) | collective-permute-done | bytes 16416 | tf_op jit(solution)/shard_map/ppermute | solution.py:25
  106.2 1.5 collective-permute-done.3
  109.2 1.0 fusion.86
  110.3 1.5 copy-done.17
  111.8 0.9 fusion.97
  113.0 1.3 convolution_bitcast_fusion
  114.3 35.6 %psum.30 = f32[4,8,128]{2,0,1:T(4,128)S(1)} all-reduce(f32[4,8,128]{2,0,1:T(4,128)S(1)} %select_bitcast_fusion), channel_id=1, replica_groups=mesh['wa'=8,'ba'=4] {'wa'}, use_global_device_ids=true, to_apply=%region_4.5 | all-reduce | flops 4096 | bytes 32768 | tf_op jit(solution)/shard_map/psum | solution.py:20
  149.9 1.1 divide_multiply_fusion
  151.1 1.3 fusion.120
  153.0 1.6 convolution_convert_fusion
  154.6 5.1 %fusion.115 = bf16[2,36,1024]{2,1,0:T(8,128)(2,1)S(1)} fusion(bf16[2,1024,320]{1,2,0:T(8,128)(2,1)} %convolution_convert_fusion, f32[2,1024,320]{1,2,0:T(8,128)S(1)} %fusion.187, f32[2,1024,320]{1,2,0:T(8,128)} %copy-done.17, f32[320]{0:T(512)S(1)} %copy-done.12, bf16[320,320]{1,0:T(8,128)(2,1)S(1)} %copy-done, bf16[320,36]{0,1:T(8,128)(2,1)S(1)} %copy-done.1), kind=kOutput, calls=%fused_computation.119 | convolution fusion | flops 482418688 | bytes 6930176 | tf_op jit(solution)/shard_map/transpose(jvp(vmap()))/dot_general | solution.py:56
  160.7 17.7 %psum.31 = f32[]{:T(128)} all-reduce(f32[]{:T(128)} %get-tuple-element.7), channel_id=1, replica_groups=mesh['wa'=8,'ba'=4] {'wa'}, use_global_device_ids=true, to_apply=%region_6.7 | all-reduce | flops 1 | bytes 8 | tf_op jit(solution)/shard_map/psum | solution.py:118
  179.2 1.3 dynamic_update_slice.14
  180.6 1.3 dynamic_update_slice.15
  182.0 2.1 %collective-permute-start.4 = (f32[4,8,128]{2,0,1:T(4,128)S(1)}, f32[4,8,128]{2,0,1:T(4,128)S(1)}, u32[]{:S(2)}, u32[]{:S(2)}) collective-permute-start(f32[4,8,128]{2,0,1:T(4,128)S(1)} %slice.235), channel_id=1, source_target_pairs={{0,4},{4,8},{8,12},{12,16},{16,20},{20,24},{24,28},{28,0},{1,5},{5... | collective-permute-start | bytes 49160 | tf_op jit(solution)/shard_map/ppermute | solution.py:25
  184.0 4.4 %collective-permute-done.4 = f32[4,8,128]{2,0,1:T(4,128)S(1)} collective-permute-done((f32[4,8,128]{2,0,1:T(4,128)S(1)}, f32[4,8,128]{2,0,1:T(4,128)S(1)}, u32[]{:S(2)}, u32[]{:S(2)}) %collective-permute-start.4) | collective-permute-done | bytes 16416 | tf_op jit(solution)/shard_map/ppermute | solution.py:25
  (117 shorter events, 10.8 us)
Async XLA Ops:
  0.0 22.0 %copy-start = (bf16[320,320]{1,0:T(8,128)(2,1)S(1)}, bf16[320,320]{1,0:T(8,128)(2,1)}, u32[]{:S(2)}) copy-start(bf16[320,320]{1,0:T(8,128)(2,1)} %param.16) | copy-start | bytes 614404
  0.8 18.9 %collective-permute-start = (f32[4,8,128]{2,0,1:T(4,128)S(1)}, f32[4,8,128]{2,0,1:T(4,128)S(1)}, u32[]{:S(2)}, u32[]{:S(2)}) collective-permute-start(f32[4,8,128]{2,0,1:T(4,128)S(1)} %get-tuple-element.43), channel_id=1, source_target_pairs={{0,28},{4,0},{8,4},{12,8},{16,12},{20,16},{24,20},{28,24},{1,29},{... | collective-permute-start | bytes 49160 | tf_op jit(solution)/shard_map/ppermute | solution.py:25
  7.6 1.1 copy-start.15
  8.1 91.2 %collective-permute-start.2 = (f32[128]{0:T(128)}, f32[128]{0:T(128)}, u32[]{:S(2)}, u32[]{:S(2)}) collective-permute-start(f32[128]{0:T(128)} %slice.200), channel_id=1, source_target_pairs={{0,4},{4,8},{8,12},{12,16},{16,20},{20,24},{24,28},{28,0},{1,5},{5... | collective-permute-start | bytes 1544 | tf_op jit(solution)/shard_map/ppermute | solution.py:25
  10.0 14.5 %copy-start.13 = (f32[320]{0:T(512)}, f32[320]{0:T(512)S(1)}, u32[]{:S(2)}) copy-start(f32[320]{0:T(512)S(1)} %get-tuple-element.6) | copy-start | bytes 3844
  22.0 2.6 %copy-start.2 = (bf16[36,320]{1,0:T(8,128)(2,1)S(1)}, bf16[36,320]{1,0:T(8,128)(2,1)}, u32[]{:S(2)}) copy-start(bf16[36,320]{1,0:T(8,128)(2,1)} %param.17) | copy-start | bytes 69124
  24.5 3.0 %copy-start.8 = (f32[64,4]{0,1:T(4,128)S(1)}, f32[64,4]{0,1:T(4,128)}, u32[]{:S(2)}) copy-start(f32[64,4]{0,1:T(4,128)} %param.19) | copy-start | bytes 3076
  66.2 1.9 %copy-start.3 = (bf16[36,320]{1,0:T(8,128)(2,1)S(1)}, bf16[36,320]{1,0:T(8,128)(2,1)}, u32[]{:S(2)}) copy-start(bf16[36,320]{1,0:T(8,128)(2,1)} %param.17) | copy-start | bytes 69124
  66.2 3.5 %copy-start.1 = (bf16[320,36]{0,1:T(8,128)(2,1)S(1)}, bf16[320,36]{0,1:T(8,128)(2,1)}, u32[]{:S(2)}) copy-start(bf16[320,36]{0,1:T(8,128)(2,1)} %param.15) | copy-start | bytes 69124
  67.6 2.2 %copy-start.14 = (f32[320]{0:T(512)S(1)}, f32[320]{0:T(512)}, u32[]{:S(2)}) copy-start(f32[320]{0:T(512)} %copy-done.13) | copy-start | bytes 3844
  69.8 29.5 %copy-start.16 = (f32[256]{0:T(256)S(1)}, f32[256]{0:T(256)}, u32[]{:S(2)}) copy-start(f32[256]{0:T(256)} %copy-done.15) | copy-start | bytes 3076
  69.8 33.9 %copy-start.7 = (f32[1,4,8,128]{3,2,1,0:T(8,128)S(1)}, f32[1,4,8,128]{3,2,1,0:T(8,128)}, u32[]{:S(2)}) copy-start(f32[1,4,8,128]{3,2,1,0:T(8,128)} %get-tuple-element.41) | copy-start | bytes 49156
  74.9 34.2 %copy-start.11 = (f32[320]{0:T(512)S(1)}, f32[320]{0:T(512)}, u32[]{:S(2)}) copy-start(f32[320]{0:T(512)} %get-tuple-element.5) | copy-start | bytes 3844
  97.2 6.5 %collective-permute-start.1 = (f32[4,8,128]{2,0,1:T(4,128)S(1)}, f32[4,8,128]{2,0,1:T(4,128)S(1)}, u32[]{:S(2)}, u32[]{:S(2)}) collective-permute-start(f32[4,8,128]{2,0,1:T(4,128)S(1)} %slice.230), channel_id=1, source_target_pairs={{0,4},{4,8},{8,12},{12,16},{16,20},{20,24},{24,28},{28,0},{1,5},{5... | collective-permute-start | bytes 49160 | tf_op jit(solution)/shard_map/ppermute | solution.py:25
  99.9 10.4 %copy-start.9 = (f32[128]{0:T(128)}, f32[128]{0:T(128)S(1)}, u32[]{:S(2)}) copy-start(f32[128]{0:T(128)S(1)} %slice_add_fusion.2) | copy-start | bytes 1540
  103.7 4.0 %collective-permute-start.3 = (f32[4,8,128]{2,0,1:T(4,128)S(1)}, f32[4,8,128]{2,0,1:T(4,128)S(1)}, u32[]{:S(2)}, u32[]{:S(2)}) collective-permute-start(f32[4,8,128]{2,0,1:T(4,128)S(1)} %divide_add_fusion.1), channel_id=1, source_target_pairs={{0,28},{4,0},{8,4},{12,8},{16,12},{20,16},{24,20},{28,24},{1,29},{... | collective-permute-start | bytes 49160 | tf_op jit(solution)/shard_map/ppermute | solution.py:25
  109.2 2.6 %copy-start.4 = (bf16[36,320]{1,0:T(8,128)(2,1)S(1)}, bf16[36,320]{1,0:T(8,128)(2,1)}, u32[]{:S(2)}) copy-start(bf16[36,320]{1,0:T(8,128)(2,1)} %param.17) | copy-start | bytes 69124
  110.2 1.5 copy-start.17
  151.0 1.9 %copy-start.5 = (bf16[36,320]{1,0:T(8,128)(2,1)S(1)}, bf16[36,320]{1,0:T(8,128)(2,1)}, u32[]{:S(2)}) copy-start(bf16[36,320]{1,0:T(8,128)(2,1)} %param.17) | copy-start | bytes 69124
  152.4 2.2 %copy-start.12 = (f32[320]{0:T(512)S(1)}, f32[320]{0:T(512)}, u32[]{:S(2)}) copy-start(f32[320]{0:T(512)} %get-tuple-element.5) | copy-start | bytes 3844
  154.6 33.9 %copy-start.6 = (f32[1,4,8,128]{3,2,1,0:T(8,128)S(1)}, f32[1,4,8,128]{3,2,1,0:T(8,128)}, u32[]{:S(2)}) copy-start(f32[1,4,8,128]{3,2,1,0:T(8,128)} %get-tuple-element.42) | copy-start | bytes 49156
  154.6 33.9 %copy-start.10 = (f32[128]{0:T(128)S(1)}, f32[128]{0:T(128)}, u32[]{:S(2)}) copy-start(f32[128]{0:T(128)} %copy-done.9) | copy-start | bytes 1540
  182.0 6.5 %collective-permute-start.4 = (f32[4,8,128]{2,0,1:T(4,128)S(1)}, f32[4,8,128]{2,0,1:T(4,128)S(1)}, u32[]{:S(2)}, u32[]{:S(2)}) collective-permute-start(f32[4,8,128]{2,0,1:T(4,128)S(1)} %slice.235), channel_id=1, source_target_pairs={{0,4},{4,8},{8,12},{12,16},{16,20},{20,24},{24,28},{28,0},{1,5},{5... | collective-permute-start | bytes 49160 | tf_op jit(solution)/shard_map/ppermute | solution.py:25
where the time goes:
time: 190 us; the launch traced here: 189 us
  blocking collectives  109 us (57%)
  matrix products  28.5 us (15%)
  local copies, waits for them, and re-layouts  14.5 us (8%)
  between operations  11.3 us (6%)
  starting transfers between devices  10.4 us (5%)
  waiting for transfers between devices  9.68 us (5%)
  other arithmetic  6.08 us (3%)
    psum x2, blocking collectives, spread_2(): return lax.psum(block, axis)  73.1 us
    psum x2, blocking collectives, window_update(): square_sum = lax.psum(jnp.sum(gradient * gradient), 'wa')  35.5 us
    dot_general x4, matrix products, denoise(): jnp.dot(w_in, stacked, preferred_element_type=jnp.float32)  12 us
    ppermute x5, starting transfers between devices, passed_along(): lax.ppermute(shard, axis, [(i, (i + by) % length) for i in range(length)])  10.4 us
    ppermute x5, waiting for transfers between devices, passed_along(): lax.ppermute(shard, axis, [(i, (i + by) % length) for i in range(length)])  9.68 us
    dot_general x4, matrix products, denoise(): jnp.dot(w_out, joined, preferred_element_type=jnp.float32)  6.77 us
    dot_general x6, matrix products, percept(): jnp.einsum('fc,chw->fhw', w_feat, cleaned, precision=lax.Precision.HIGHEST)  6.17 us
    dynamic_update_slice x4, local copies, waits for them, and re-layouts, window_update(): lax.dynamic_update_slice_in_dim(summed, current + advanced[index], starts...  5.25 us
  transfers between devices with their start and end apart: 5, of which 3 were waited for; matrix products, arithmetic and copies ran while one was open for 15% of the time, Pallas kernels for 0%

commit v1 on v0

v1 whole, which is shorter than its diff:
```python
import functools
import math

import jax
import jax.numpy as jnp
from jax import lax
from jax.experimental import pallas as pl
from jax.experimental.pallas import tpu as pltpu
from jax.sharding import PartitionSpec as P

WIN = 128
STRIDE = 64
CHUNK = 256

TAP_SHIFTS = ((-1, -1), (-1, 0), (-1, 1), (0, -1), (0, 0), (0, 1), (1, -1), (1, 0), (1, 1))
CUMULATIVE_ALPHA = (0.35, 0.55, 0.72, 0.85, 0.93)
STABILITY = 1e-06
F32 = jnp.float32
BF16 = jnp.bfloat16


def plan(number):
    current = CUMULATIVE_ALPHA[number]
    following = CUMULATIVE_ALPHA[number + 1]
    spread = 0.3 * math.sqrt(1.0 - following)
    return (
        math.sqrt(current),
        math.sqrt(1.0 - current),
        math.sqrt(following),
        math.sqrt(1.0 - following - spread * spread),
        spread,
    )


def mm(a, b):
    return jnp.dot(a, b, preferred_element_type=F32)


def mm_nt(a, b):
    return lax.dot_general(a, b, (((1,), (1,)), ((), ())), preferred_element_type=F32)


def silu_pair(v):
    s = 0.5 * jnp.tanh(0.5 * v) + 0.5
    a = v * s
    return a, s + a * (1.0 - s)


def kernel(
    n, steps, per_dev, channels, height, width, hid, feat,
    latent_ref, noise_ref, offsets_ref, anchors_ref, guidance_ref,
    w_in_ref, w_mid_ref, w_out_ref, t_embed_ref, w_feat_ref,
    out_ref,
    wi, wit, wo, wot, wmt, emb, wfb,
    taps, outward, deriv_h, deriv_m, clean_ref, per_a, per_d, dclean_ref,
    init_src, init_dst, cover_src, cover_dst,
    anchor_buf, square_buf, own_src, own_dst, spill_src, spill_dst,
    init_send, init_recv, anchor_send, anchor_recv, square_send, square_recv, edge_send, edge_recv,
):
    me = lax.axis_index("wa")
    right, left = lax.rem(me + 1, n), lax.rem(me + n - 1, n)
    rows = per_dev * channels
    flat = height * width
    nine = len(TAP_SHIFTS)

    barrier = pltpu.get_barrier_semaphore()

    def greet(d, carry):
        pl.semaphore_signal(
            barrier, inc=1, device_id={"wa": lax.rem(me + d, n)},
            device_id_type=pl.DeviceIdType.MESH,
        )
        return carry

    lax.fori_loop(1, n, greet, 0)

    def remote(src, dst, send_sem, recv_sem, target):
        return pltpu.make_async_remote_copy(
            src_ref=src, dst_ref=dst, send_sem=send_sem, recv_sem=recv_sem,
            device_id={"wa": target}, device_id_type=pl.DeviceIdType.MESH,
        )

    def to_all(buf, send_sem, recv_sem):
        def one(d, carry):
            remote(buf.at[0], buf.at[d], send_sem, recv_sem, lax.rem(me + d, n)).start()
            return carry

        lax.fori_loop(1, n, one, 0)

    def await_all(buf, sem):
        rest = buf.at[pl.ds(1, n - 1)]
        pltpu.make_async_copy(rest, rest, sem).wait()

    lane = lax.broadcasted_iota(jnp.int32, (rows, width), 1)
    row = lax.broadcasted_iota(jnp.int32, (rows, width), 0)
    first = row < channels
    row_all = lax.broadcasted_iota(jnp.int32, (rows, flat), 0)
    starts = [offsets_ref[i] + i * STRIDE for i in range(per_dev)]
    start_row = jnp.where(first, starts[0], starts[1])
    keep = lane >= start_row

    def tiles(value):
        return [value[:, h * width : (h + 1) * width] for h in range(height)]

    def joined_tiles(parts):
        return jnp.concatenate(parts, axis=1)

    def from_right(x):
        return jnp.where(lane == width - 1, 0.0, pltpu.roll(x, width - 1, 1))

    def from_left(x):
        return jnp.where(lane == 0, 0.0, pltpu.roll(x, 1, 1))

    def expand(parts, sign):
        moved = {0: parts, 1: [from_right(p) for p in parts], -1: [from_left(p) for p in parts]}
        zero = jnp.zeros((rows, width), F32)
        blocks = []
        for down, across in TAP_SHIFTS:
            source = moved[sign * across]
            blocks.append(
                joined_tiles(
                    [
                        source[h + sign * down] if 0 <= h + sign * down < height else zero
                        for h in range(height)
                    ]
                )
            )
        return jnp.concatenate(blocks, axis=0).astype(BF16)

    def collapse(ref, sign):
        result = []
        for h in range(height):
            sums = {}
            for k, (down, across) in enumerate(TAP_SHIFTS):
                source = h + sign * down
                if 0 <= source < height:
                    piece = ref[k * rows : (k + 1) * rows, source * width : (source + 1) * width]
                    key = sign * across
                    sums[key] = sums[key] + piece if key in sums else piece
            result.append(sums[0] + from_right(sums[1]) + from_left(sums[-1]))
        return result

    def half_swap(x):
        return pltpu.roll(x, channels, 0)

    for h in range(height):
        cols = slice(h * width, (h + 1) * width)
        init_src[0:channels, cols] = latent_ref[:, h, :]
        for s in range(steps - 1):
            init_src[(s + 1) * channels : (s + 2) * channels, cols] = noise_ref[s, :, h, :]
    own_cover = jnp.zeros((rows, width), F32)
    for i in range(per_dev):
        own_cover = own_cover + (lane >= starts[i]).astype(F32)
    spill_cover = per_dev - own_cover
    cover_src[0] = own_cover
    cover_src[1] = spill_cover

    pl.semaphore_wait(barrier, n - 1)
    init_copy = remote(init_src, init_dst, init_send.at[0], init_recv.at[0], left)
    cover_left = remote(cover_src.at[0], cover_dst.at[0], init_send.at[1], init_recv.at[1], left)
    cover_right = remote(cover_src.at[1], cover_dst.at[1], init_send.at[2], init_recv.at[2], right)
    init_copy.start()
    cover_left.start()
    cover_right.start()

    w_in = w_in_ref[...]
    w_out = w_out_ref[...]
    small = nine * channels
    eye_r = lax.broadcasted_iota(jnp.int32, (hid, hid), 0)
    eye_c = lax.broadcasted_iota(jnp.int32, (hid, hid), 1)
    eye = eye_r == eye_c
    eye_b = jnp.where(eye, 1.0, 0.0).astype(BF16)
    wmt[...] = mm_nt(eye_b, w_mid_ref[...]).astype(BF16)
    w_out_t = mm_nt(eye_b, w_out).astype(BF16)
    for i in range(per_dev):
        def hot(a, b):
            return jnp.where((a // channels) * rows + i * channels + a % channels == b, 1.0, 0.0).astype(BF16)

        spot = hot(
            lax.broadcasted_iota(jnp.int32, (small, nine * rows), 0),
            lax.broadcasted_iota(jnp.int32, (small, nine * rows), 1),
        )
        spot_t = hot(
            lax.broadcasted_iota(jnp.int32, (nine * rows, small), 1),
            lax.broadcasted_iota(jnp.int32, (nine * rows, small), 0),
        )
        wi[i] = mm(w_in, spot).astype(BF16)
        wit[i] = mm_nt(spot_t, w_in).astype(BF16)
        wo[i] = mm(spot_t, w_out).astype(BF16)
        wot[i] = mm(w_out_t, spot).astype(BF16)
    for s in range(steps):
        column = jnp.sum(jnp.where(eye, t_embed_ref[s : s + 1, :], 0.0), axis=1, keepdims=True)
        emb[s] = jnp.broadcast_to(column, (hid, WIN))
    for c in range(channels):
        wfb[c] = jnp.broadcast_to(w_feat_ref[:, c : c + 1], (feat, width))

    cover_left.wait()
    cover_right.wait()
    count_own = own_cover + cover_dst[1]
    count_next = cover_dst[0] + spill_cover
    init_copy.wait()

    def doubled(value):
        return jnp.concatenate([value] * per_dev, axis=0)

    state = tiles(doubled(init_src[0:channels, :]))
    state_next = tiles(doubled(init_dst[0:channels, :]))

    for s in range(steps):
        now_a, now_s, next_a, direction, spread = plan(s)
        last = s == steps - 1

        window = []
        for h in range(height):
            cut = [
                pltpu.roll(jnp.where(lane >= start, state[h], state_next[h]), width - start, 1)
                for start in starts
            ]
            window.append(jnp.where(first, cut[0], cut[1]))
        taps[...] = expand(window, 1)

        def forward(j, carry):
            cols = pl.ds(pl.multiple_of(j * CHUNK, CHUNK), CHUNK)
            stacked = taps[:, cols]
            shift = jnp.concatenate([emb[s]] * (CHUNK // WIN), axis=1)
            total = None
            for i in range(per_dev):
                hidden = mm(wi[i], stacked) + shift
                act, slope = silu_pair(hidden)
                deriv_h[i, :, cols] = slope
                middle = mm(w_mid_ref[...], act.astype(BF16))
                act2, slope2 = silu_pair(middle)
                deriv_m[i, :, cols] = slope2
                piece = mm(wo[i], (hidden + act2).astype(BF16))
                total = piece if total is None else total + piece
            outward[:, cols] = total
            return carry

        lax.fori_loop(0, flat // CHUNK, forward, 0)

        predicted = collapse(outward, 1)
        cleaned = [(window[h] - now_s * predicted[h]) * (1.0 / now_a) for h in range(height)]
        clean_all = joined_tiles(cleaned)
        clean_ref[...] = clean_all
        chosen = jnp.where(row_all // channels + me * per_dev == anchors_ref[s], clean_all, 0.0)
        chosen = chosen + half_swap(chosen)
        anchor_buf[s, 0] = chosen[0:channels, :]
        to_all(anchor_buf.at[s], anchor_send.at[s], anchor_recv.at[s])

        def percept_of(source, base):
            value = wfb[0] * source[base : base + 1, :]
            for c in range(1, channels):
                value = value + wfb[c] * source[base + c : base + c + 1, :]
            return value

        def features(h, carry):
            cols = pl.ds(pl.multiple_of(h * width, width), width)
            source = clean_ref[:, cols]
            for i in range(per_dev):
                act, slope = silu_pair(percept_of(source, i * channels))
                per_a[i, :, cols] = act
                per_d[i, :, cols] = slope
            return carry

        lax.fori_loop(0, height, features, 0)

        await_all(anchor_buf.at[s], anchor_recv.at[s])

        def backward_features(h, carry):
            cols = pl.ds(pl.multiple_of(h * width, width), width)
            anchor = anchor_buf[s, 0, :, cols]
            for d in range(1, n):
                anchor = anchor + anchor_buf[s, d, :, cols]
            anchor_act = silu_pair(percept_of(anchor, 0))[0]
            lines = []
            for i in range(per_dev):
                slope = (per_a[i, :, cols] - anchor_act) * (1.0 / feat) * per_d[i, :, cols]
                for c in range(channels):
                    lines.append(jnp.sum(wfb[c] * slope, axis=0, keepdims=True))
            dclean_ref[:, cols] = jnp.concatenate(lines, axis=0)
            return carry

        lax.fori_loop(0, height, backward_features, 0)

        dclean = tiles(dclean_ref[...])
        taps[...] = expand([(-now_s / now_a) * d for d in dclean], -1)

        def backward(j, carry):
            cols = pl.ds(pl.multiple_of(j * CHUNK, CHUNK), CHUNK)
            stacked = taps[:, cols]
            total = None
            for i in range(per_dev):
                d_joined = mm(wot[i], stacked).astype(BF16).astype(F32)
                d_middle = (d_joined * deriv_m[i, :, cols]).astype(BF16)
                d_act = mm(wmt[...], d_middle).astype(BF16).astype(F32)
                d_hidden = (d_joined + d_act * deriv_h[i, :, cols]).astype(BF16)
                piece = mm(wit[i], d_hidden)
                total = piece if total is None else total + piece
            outward[:, cols] = total.astype(BF16).astype(F32)
            return carry

        lax.fori_loop(0, flat // CHUNK, backward, 0)

        through = collapse(outward, -1)
        gradient = [
            dclean[h] * (1.0 / now_a) + through[h].astype(BF16).astype(F32) for h in range(height)
        ]
        square = gradient[0] * gradient[0]
        for h in range(1, height):
            square = square + gradient[h] * gradient[h]
        square_buf[s, 0] = square
        to_all(square_buf.at[s], square_send.at[s], square_recv.at[s])

        def placed(x):
            moved = jnp.where(first, pltpu.roll(x, starts[0], 1), pltpu.roll(x, starts[1], 1))
            own = jnp.where(keep, moved, 0.0)
            over = moved - own
            return own + half_swap(own), over + half_swap(over)

        own_parts, spill_parts = [], []
        for h in range(height):
            base = (next_a / now_a) * (window[h] - now_s * predicted[h]) + direction * predicted[h]
            base_own, base_over = placed(base)
            grad_own, grad_over = placed(gradient[h])
            own_parts.append(jnp.where(first, base_own, grad_own))
            spill_parts.append(jnp.where(first, base_over, grad_over))
        spill_src[s] = joined_tiles(spill_parts)
        to_right = remote(spill_src.at[s], spill_dst.at[s], edge_send.at[2 * s], edge_recv.at[2 * s], right)
        to_right.start()
        if not last:
            own_src[s] = joined_tiles(own_parts)
            to_left = remote(own_src.at[s], own_dst.at[s], edge_send.at[2 * s + 1], edge_recv.at[2 * s + 1], left)
            to_left.start()

        def merged(own, spill, coef, count, noise):
            both = own + spill
            swapped = half_swap(both)
            base = jnp.where(first, both, swapped)
            grad = jnp.where(first, swapped, both)
            return (base - coef * grad) / count + spread * noise

        await_all(square_buf.at[s], square_recv.at[s])
        square = square_buf[s, 0]
        for d in range(1, n):
            square = square + square_buf[s, d]
        mean = jnp.sum(jnp.sum(square, axis=0, keepdims=True), axis=1, keepdims=True) * (
            1.0 / (n * rows * flat)
        )
        coef = (next_a / now_a) * guidance_ref[0] * lax.rsqrt(
            jnp.broadcast_to(mean, (rows, width)) + STABILITY
        )
        to_right.wait()
        spill = tiles(spill_dst[s])
        if last:
            for h in range(height):
                noise = doubled(noise_ref[s, :, h, :])
                out_ref[:, h, :] = merged(own_parts[h], spill[h], coef, count_own, noise)[0:channels, :]
        else:
            to_left.wait()
            noise_own = tiles(doubled(init_src[(s + 1) * channels : (s + 2) * channels, :]))
            noise_next = tiles(doubled(init_dst[(s + 1) * channels : (s + 2) * channels, :]))
            arrived = tiles(own_dst[s])
            state = [
                merged(own_parts[h], spill[h], coef, count_own, noise_own[h]) for h in range(height)
            ]
            state_next = [
                merged(arrived[h], spill_parts[h], coef, count_next, noise_next[h])
                for h in range(height)
            ]

    for s in range(steps):
        await_all(anchor_buf.at[s], anchor_send.at[s])
        await_all(square_buf.at[s], square_send.at[s])


def local(n, latent, noise, offsets, anchors, guidance, w_in, w_mid, w_out, t_embed, w_feat):
    channels, height, width = latent.shape
    per_dev = offsets.shape[0]
    steps = t_embed.shape[0]
    hid = w_mid.shape[0]
    feat = w_feat.shape[0]
    rows = per_dev * channels
    assert width == WIN and per_dev == 2
    flat = height * width
    tall = len(TAP_SHIFTS) * rows
    vmem = pl.BlockSpec(memory_space=pltpu.VMEM)
    smem = pl.BlockSpec(memory_space=pltpu.SMEM)
    dma = pltpu.SemaphoreType.DMA
    return pl.pallas_call(
        functools.partial(kernel, n, steps, per_dev, channels, height, width, hid, feat),
        out_shape=jax.ShapeDtypeStruct(latent.shape, F32),
        in_specs=[vmem, vmem, smem, smem, smem, vmem, vmem, vmem, vmem, vmem],
        out_specs=vmem,
        scratch_shapes=[
            pltpu.VMEM((per_dev, hid, tall), BF16),
            pltpu.VMEM((per_dev, tall, hid), BF16),
            pltpu.VMEM((per_dev, tall, hid), BF16),
            pltpu.VMEM((per_dev, hid, tall), BF16),
            pltpu.VMEM((hid, hid), BF16),
            pltpu.VMEM((steps, hid, WIN), F32),
            pltpu.VMEM((channels, feat, width), F32),
            pltpu.VMEM((tall, flat), BF16),
            pltpu.VMEM((tall, flat), F32),
            pltpu.VMEM((per_dev, hid, flat), F32),
            pltpu.VMEM((per_dev, hid, flat), F32),
            pltpu.VMEM((rows, flat), F32),
            pltpu.VMEM((per_dev, feat, flat), F32),
            pltpu.VMEM((per_dev, feat, flat), F32),
            pltpu.VMEM((rows, flat), F32),
            pltpu.VMEM((steps * channels, flat), F32),
            pltpu.VMEM((steps * channels, flat), F32),
            pltpu.VMEM((2, rows, width), F32),
            pltpu.VMEM((2, rows, width), F32),
            pltpu.VMEM((steps, n, channels, flat), F32),
            pltpu.VMEM((steps, n, rows, width), F32),
            pltpu.VMEM((steps, rows, flat), F32),
            pltpu.VMEM((steps, rows, flat), F32),
            pltpu.VMEM((steps, rows, flat), F32),
            pltpu.VMEM((steps, rows, flat), F32),
            dma((3,)),
            dma((3,)),
            dma((steps,)),
            dma((steps,)),
            dma((steps,)),
            dma((steps,)),
            dma((2 * steps,)),
            dma((2 * steps,)),
        ],
        compiler_params=pltpu.CompilerParams(
            collective_id=0, has_side_effects=True, vmem_limit_bytes=48 * 1024 * 1024
        ),
        name="panorama",
    )(latent, noise, offsets, anchors, guidance, w_in, w_mid, w_out, t_embed, w_feat)


def solution(mesh):
    return jax.shard_map(
        functools.partial(local, mesh.shape["wa"]),
        mesh=mesh,
        in_specs=(
            P("ba", None, "wa"),
            P(None, "ba", None, "wa"),
            P("wa"),
            P(),
            P(),
            P(),
            P(),
            P(),
            P(),
            P(),
        ),
        out_specs=P("ba", None, "wa"),
        check_vma=False,
    )
```

time: 190 us -> 47.6 us (0.25)
  blocking collectives: 109 us -> 0 us
  Pallas kernels: 0 us -> 43.5 us
  matrix products: 28.5 us -> 0 us
  local copies, waits for them, and re-layouts: 14.5 us -> 3.05 us
  between operations: 11.3 us -> 0.73 us
  starting transfers between devices: 10.4 us -> 0 us
  waiting for transfers between devices: 9.68 us -> 0 us
  other arithmetic: 6.08 us -> 0 us
    psum x4 -> x0, blocking collectives: 109 us -> none  [the longest x2 73.1 us: spread_2(): return lax.psum(block, axis)]
    pallas_call x0 -> x1, Pallas kernels: none -> 43.5 us  [local(): pl.pallas_call(functools.partial(kernel, n, steps, per_dev, channels, hei...]
    dot_general x16 -> x0, matrix products: 28.5 us -> none  [the longest x4 12 us: denoise(): jnp.dot(w_in, stacked, preferred_element_type=jnp.float32)]
    ppermute x5 -> x0, starting transfers between devices: 10.4 us -> none  [passed_along(): lax.ppermute(shard, axis, [(i, (i + by) % length) for i in range(length)])]
    ppermute x5 -> x0, waiting for transfers between devices: 9.68 us -> none  [passed_along(): lax.ppermute(shard, axis, [(i, (i + by) % length) for i in range(length)])]
    dynamic_update_slice x4 -> x0, local copies, waits for them, and re-layouts: 5.25 us -> none  [window_update(): lax.dynamic_update_slice_in_dim(summed, current + advanced[index], starts...]
    slice x6 -> x0, local copies, waits for them, and re-layouts: 3.77 us -> none  [the longest x1 1.35 us: window_update(): embedding = t_embed[number]]
  transfers between devices with their start and end apart: 5 -> 0, of which waited for: 3 -> 0; matrix products, arithmetic and copies ran while one was open for 15% -> 0% of each run, Pallas kernels for 0% -> 0%
where the time goes in v1:
time: 47.6 us; the launch traced here: 47.3 us
  Pallas kernels  43.5 us (91%)
  local copies, waits for them, and re-layouts  3.05 us (6%)
  between operations  0.73 us (2%)
    pallas_call x1, Pallas kernels, local(): pl.pallas_call(functools.partial(kernel, n, steps, per_dev, channels, hei...  43.5 us
    unnamed x19, local copies, waits for them, and re-layouts  3.05 us

profile of v1, /device:TPU:0, one launch (start us, length us, event | category | flops | bytes accessed | tf_op | source)
XLA Modules:
  0.0 47.3 jit_solution(13576880446328556011)
XLA Ops:
  0.0 0.0 copy-start.7
  0.7 0.8 %copy.12.w_feat_ref = f32[64,4]{1,0:T(8,128)S(1)} copy(f32[64,4]{0,1:T(4,128)} %param.19) | data formatting | bytes 2048 | tf_op args[9]
  1.4 0.0 copy-done.7
  1.4 0.0 copy-start.1
  1.4 0.0 copy-start.2
  1.5 0.0 copy-start.3
  1.5 0.0 copy-start.4
  1.5 0.0 copy-start.5
  1.5 0.0 copy-start.6
  1.5 0.1 copy.11.w_in_ref
  1.6 0.6 %copy-done.1 = f32[2,4,8,128]{3,2,1,0:T(8,128)S(1)} copy-done((f32[2,4,8,128]{3,2,1,0:T(8,128)S(1)}, f32[2,4,8,128]{3,2,1,0:T(8,128)}, u32[]{:S(2)}) %copy-start.1) | copy-done | bytes 32792
  2.2 0.0 copy-done.2
  2.2 0.0 copy-done.3
  2.2 0.0 copy-done.4
  2.2 0.0 copy-done.5
  2.2 0.0 copy-done.6
  2.2 0.0 copy-start
  2.2 0.9 %copy-done = bf16[320,320]{1,0:T(8,128)(2,1)S(1)} copy-done((bf16[320,320]{1,0:T(8,128)(2,1)S(1)}, bf16[320,320]{1,0:T(8,128)(2,1)}, u32[]{:S(2)}) %copy-start) | copy-done | bytes 204824
  3.2 43.5 %panorama.1 = f32[4,8,128]{2,1,0:T(8,128)S(1)} custom-call(f32[4,8,128]{2,1,0:T(8,128)S(1)} %copy-done.3, f32[2,4,8,128]{3,2,1,0:T(8,128)S(1)} %copy-done.1, s32[2]{0:T(128)S(1)} %copy-done.5, s32[2]{0:T(128)S(1)} %copy-done.6, f32[1]{0:T(128)S(6)} %copy.14.guidance_ref, bf16[320,36]{1,0:T(8,128)(2,1)S(1)} %copy.11.w_in_ref, bf16[320,320]{1,0:T(8,128)(2,1)S(1)} %copy-done, ...), custom_call_target="tpu_custom_call" | custom-call | tf_op jit(solution)/shard_map/panorama/pallas_call | solution.py:389
  46.7 0.6 %copy.15 = f32[4,8,128]{2,1,0:T(8,128)} copy(f32[4,8,128]{2,1,0:T(8,128)S(1)} %panorama.1) | data formatting | bytes 32768
Async XLA Ops:
  0.0 1.4 %copy-start.7 = (bf16[320,36]{0,1:T(8,128)(2,1)S(1)}, bf16[320,36]{0,1:T(8,128)(2,1)}, u32[]{:S(2)}) copy-start(bf16[320,36]{0,1:T(8,128)(2,1)} %param.15) | copy-start | bytes 69124
  1.4 0.8 %copy-start.1 = (f32[2,4,8,128]{3,2,1,0:T(8,128)S(1)}, f32[2,4,8,128]{3,2,1,0:T(8,128)}, u32[]{:S(2)}) copy-start(f32[2,4,8,128]{3,2,1,0:T(8,128)} %noise_ref.1) | copy-start | bytes 98308
  1.4 0.8 %copy-start.2 = (bf16[36,320]{1,0:T(8,128)(2,1)S(1)}, bf16[36,320]{1,0:T(8,128)(2,1)}, u32[]{:S(2)}) copy-start(bf16[36,320]{1,0:T(8,128)(2,1)} %w_out_ref.1) | copy-start | bytes 69124
  1.5 0.8 %copy-start.3 = (f32[4,8,128]{2,1,0:T(8,128)S(1)}, f32[4,8,128]{2,1,0:T(8,128)}, u32[]{:S(2)}) copy-start(f32[4,8,128]{2,1,0:T(8,128)} %latent_ref.1) | copy-start | bytes 49156
  1.5 0.7 %copy-start.4 = (f32[2,320]{1,0:T(2,128)S(1)}, f32[2,320]{1,0:T(2,128)}, u32[]{:S(2)}) copy-start(f32[2,320]{1,0:T(2,128)} %t_embed_ref.1) | copy-start | bytes 7684
  1.5 0.7 %copy-start.5 = (s32[2]{0:T(128)S(1)}, s32[2]{0:T(128)}, u32[]{:S(2)}) copy-start(s32[2]{0:T(128)} %offsets_ref.1) | copy-start | bytes 28
  1.5 0.7 %copy-start.6 = (s32[2]{0:T(128)S(1)}, s32[2]{0:T(128)}, u32[]{:S(2)}) copy-start(s32[2]{0:T(128)} %anchors_ref.1) | copy-start | bytes 28
  2.2 0.9 %copy-start = (bf16[320,320]{1,0:T(8,128)(2,1)S(1)}, bf16[320,320]{1,0:T(8,128)(2,1)}, u32[]{:S(2)}) copy-start(bf16[320,320]{1,0:T(8,128)(2,1)} %w_mid_ref.1) | copy-start | bytes 614404

commit v2 on v1

--- a/solution.py
+++ b/solution.py
@@ -11,6 +11,7 @@
 WIN = 128
 STRIDE = 64
 CHUNK = 256
+SIDE = 2
 
 TAP_SHIFTS = ((-1, -1), (-1, 0), (-1, 1), (0, -1), (0, 0), (0, 1), (1, -1), (1, 0), (1, 1))
 CUMULATIVE_ALPHA = (0.35, 0.55, 0.72, 0.85, 0.93)
@@ -46,15 +47,25 @@
     return a, s + a * (1.0 - s)
 
 
+def silu_half(u):
+    t = jnp.tanh(u)
+    a = u * (t + 1.0)
+    low, act = t.astype(BF16), a.astype(BF16)
+    return u, a, (low + 1.0) + act * (1.0 - low)
+
+
 def kernel(
     n, steps, per_dev, channels, height, width, hid, feat,
+    latent_hbm, noise_hbm, offsets_hbm, anchors_hbm, guidance_hbm,
+    w_in_hbm, w_mid_hbm, w_out_hbm, t_embed_hbm, w_feat_hbm,
+    out_ref,
     latent_ref, noise_ref, offsets_ref, anchors_ref, guidance_ref,
-    w_in_ref, w_mid_ref, w_out_ref, t_embed_ref, w_feat_ref,
-    out_ref,
-    wi, wit, wo, wot, wmt, emb, wfb,
+    w_in_ref, w_mid_ref, w_out_ref, t_embed_ref, w_feat_ref, load_sem,
+    wi, wit, wo, wot, wm, wmt, wfb,
     taps, outward, deriv_h, deriv_m, clean_ref, per_a, per_d, dclean_ref,
     init_src, init_dst, cover_src, cover_dst,
-    anchor_buf, square_buf, own_src, own_dst, spill_src, spill_dst,
+    anchor_buf, square_buf, own_base, own_base_in, spill_base, spill_base_in,
+    own_grad, own_grad_in, spill_grad, spill_grad_in,
     init_send, init_recv, anchor_send, anchor_recv, square_send, square_recv, edge_send, edge_recv,
 ):
     me = lax.axis_index("wa")
@@ -74,6 +85,28 @@
 
     lax.fori_loop(1, n, greet, 0)
 
+    loads = [
+        pltpu.make_async_copy(src, dst, load_sem.at[k])
+        for k, (src, dst) in enumerate(
+            (
+                (latent_hbm, latent_ref),
+                (noise_hbm, noise_ref),
+                (offsets_hbm, offsets_ref),
+                (w_mid_hbm, w_mid_ref),
+                (w_in_hbm, w_in_ref),
+                (w_out_hbm, w_out_ref),
+                (t_embed_hbm, t_embed_ref),
+                (w_feat_hbm, w_feat_ref),
+                (anchors_hbm, anchors_ref),
+                (guidance_hbm, guidance_ref),
+            )
+        )
+    ]
+    for load in loads:
+        load.start()
+    for load in loads[:3]:
+        load.wait()
+
     def remote(src, dst, send_sem, recv_sem, target):
         return pltpu.make_async_remote_copy(
             src_ref=src, dst_ref=dst, send_sem=send_sem, recv_sem=recv_sem,
@@ -94,10 +127,9 @@
     lane = lax.broadcasted_iota(jnp.int32, (rows, width), 1)
     row = lax.broadcasted_iota(jnp.int32, (rows, width), 0)
     first = row < channels
-    row_all = lax.broadcasted_iota(jnp.int32, (rows, flat), 0)
     starts = [offsets_ref[i] + i * STRIDE for i in range(per_dev)]
-    start_row = jnp.where(first, starts[0], starts[1])
-    keep = lane >= start_row
+
+    ones = jnp.where(lax.broadcasted_iota(jnp.int32, (rows, flat), 0) < 3, 1.0, 0.0)
 
     def tiles(value):
         return [value[:, h * width : (h + 1) * width] for h in range(height)]
@@ -125,6 +157,7 @@
                     ]
                 )
             )
+        blocks.append(ones)
         return jnp.concatenate(blocks, axis=0).astype(BF16)
 
     def collapse(ref, sign):
@@ -163,36 +196,53 @@
     cover_left.start()
     cover_right.start()
 
-    w_in = w_in_ref[...]
+    for load in loads[3:]:
+        load.wait()
+
+    w_in_t = w_in_ref[...]
     w_out = w_out_ref[...]
     small = nine * channels
     eye_r = lax.broadcasted_iota(jnp.int32, (hid, hid), 0)
     eye_c = lax.broadcasted_iota(jnp.int32, (hid, hid), 1)
     eye = eye_r == eye_c
     eye_b = jnp.where(eye, 1.0, 0.0).astype(BF16)
-    wmt[...] = mm_nt(eye_b, w_mid_ref[...]).astype(BF16)
+    wm[...] = (0.5 * w_mid_ref[...].astype(F32)).astype(BF16)
+    wmt[...] = (0.25 * mm_nt(eye_b, w_mid_ref[...])).astype(BF16)
     w_out_t = mm_nt(eye_b, w_out).astype(BF16)
+    w_in = mm_nt(eye_b, w_in_t).astype(BF16)
+    place = lax.broadcasted_iota(jnp.int32, (hid, (nine + 1) * rows), 1)
+    embeds = []
+    for s in range(steps):
+        rest = 0.5 * jnp.sum(jnp.where(eye, t_embed_ref[s : s + 1, :], 0.0), axis=1, keepdims=True)
+        spread_out = jnp.zeros((hid, (nine + 1) * rows), F32)
+        for k in range(3):
+            term = rest.astype(BF16).astype(F32)
+            spread_out = jnp.where(place == nine * rows + k, term, spread_out)
+            rest = rest - term
+        embeds.append(spread_out)
     for i in range(per_dev):
         def hot(a, b):
             return jnp.where((a // channels) * rows + i * channels + a % channels == b, 1.0, 0.0).astype(BF16)
 
         spot = hot(
-            lax.broadcasted_iota(jnp.int32, (small, nine * rows), 0),
-            lax.broadcasted_iota(jnp.int32, (small, nine * rows), 1),
+            lax.broadcasted_iota(jnp.int32, (small, (nine + 1) * rows), 0),
+            lax.broadcasted_iota(jnp.int32, (small, (nine + 1) * rows), 1),
         )
         spot_t = hot(
             lax.broadcasted_iota(jnp.int32, (nine * rows, small), 1),
             lax.broadcasted_iota(jnp.int32, (nine * rows, small), 0),
         )
-        wi[i] = mm(w_in, spot).astype(BF16)
-        wit[i] = mm_nt(spot_t, w_in).astype(BF16)
+        taken = 0.5 * mm(w_in, spot)
+        for s in range(steps):
+            wi[s, i] = (taken + embeds[s]).astype(BF16)
+        wit[i] = mm(spot_t, w_in_t).astype(BF16)
         wo[i] = mm(spot_t, w_out).astype(BF16)
         wot[i] = mm(w_out_t, spot).astype(BF16)
-    for s in range(steps):
-        column = jnp.sum(jnp.where(eye, t_embed_ref[s : s + 1, :], 0.0), axis=1, keepdims=True)
-        emb[s] = jnp.broadcast_to(column, (hid, WIN))
     for c in range(channels):
-        wfb[c] = jnp.broadcast_to(w_feat_ref[:, c : c + 1], (feat, width))
+        column = jnp.sum(
+            jnp.where(eye[0:feat, 0:feat], w_feat_ref[c : c + 1, :], 0.0), axis=1, keepdims=True
+        )
+        wfb[c] = jnp.broadcast_to(column, (feat, width))
 
     cover_left.wait()
     cover_right.wait()
@@ -200,6 +250,9 @@
     count_next = cover_dst[0] + spill_cover
     init_copy.wait()
 
+    def all_tiles(count):
+        return jnp.concatenate([count[0:channels]] * height, axis=1)
+
     def doubled(value):
         return jnp.concatenate([value] * per_dev, axis=0)
 
@@ -209,43 +262,45 @@
     for s in range(steps):
         now_a, now_s, next_a, direction, spread = plan(s)
         last = s == steps - 1
+        slot = lax.rem(anchors_ref[s], per_dev)
+        owner = lax.div(anchors_ref[s], per_dev)
+        order = [jnp.where(slot == 0, starts[0], starts[1]), jnp.where(slot == 0, starts[1], starts[0])]
+        keep = lane >= jnp.where(first, order[0], order[1])
 
         window = []
         for h in range(height):
             cut = [
                 pltpu.roll(jnp.where(lane >= start, state[h], state_next[h]), width - start, 1)
-                for start in starts
+                for start in order
             ]
             window.append(jnp.where(first, cut[0], cut[1]))
         taps[...] = expand(window, 1)
 
-        def forward(j, carry):
-            cols = pl.ds(pl.multiple_of(j * CHUNK, CHUNK), CHUNK)
-            stacked = taps[:, cols]
-            shift = jnp.concatenate([emb[s]] * (CHUNK // WIN), axis=1)
-            total = None
-            for i in range(per_dev):
-                hidden = mm(wi[i], stacked) + shift
-                act, slope = silu_pair(hidden)
-                deriv_h[i, :, cols] = slope
-                middle = mm(w_mid_ref[...], act.astype(BF16))
-                act2, slope2 = silu_pair(middle)
-                deriv_m[i, :, cols] = slope2
-                piece = mm(wo[i], (hidden + act2).astype(BF16))
-                total = piece if total is None else total + piece
-            outward[:, cols] = total
-            return carry
-
-        lax.fori_loop(0, flat // CHUNK, forward, 0)
-
-        predicted = collapse(outward, 1)
-        cleaned = [(window[h] - now_s * predicted[h]) * (1.0 / now_a) for h in range(height)]
+        def forward(i):
+            def block(j, carry):
+                for part in range(SIDE):
+                    cols = pl.ds(pl.multiple_of((j * SIDE + part) * CHUNK, CHUNK), CHUNK)
+                    stacked = taps[:, cols]
+                    half, act, slope = silu_half(mm(wi[s, i], stacked))
+                    act = act.astype(BF16)
+                    deriv_h[i, :, cols] = slope
+                    act2, slope2 = silu_half(mm(wm[...], act))[1:]
+                    deriv_m[i, :, cols] = slope2
+                    piece = mm(wo[i], ((half + half) + act2).astype(BF16))
+                    outward[:, cols] = piece if i == 0 else outward[:, cols] + piece
+                return carry
+
+            lax.fori_loop(0, flat // (CHUNK * SIDE), block, 0)
+            predicted = collapse(outward, 1)
+            cleaned = [(window[h] - now_s * predicted[h]) * (1.0 / now_a) for h in range(height)]
+            return predicted, cleaned
+
+        cleaned = forward(0)[1]
+        anchor_buf[s, 0] = jnp.where(owner == me, joined_tiles(cleaned)[0:channels, :], 0.0)
+        to_all(anchor_buf.at[s], anchor_send.at[s], anchor_recv.at[s])
+        predicted, cleaned = forward(1)
         clean_all = joined_tiles(cleaned)
         clean_ref[...] = clean_all
-        chosen = jnp.where(row_all // channels + me * per_dev == anchors_ref[s], clean_all, 0.0)
-        chosen = chosen + half_swap(chosen)
-        anchor_buf[s, 0] = chosen[0:channels, :]
-        to_all(anchor_buf.at[s], anchor_send.at[s], anchor_recv.at[s])
 
         def percept_of(source, base):
             value = wfb[0] * source[base : base + 1, :]
@@ -263,6 +318,30 @@
             return carry
 
         lax.fori_loop(0, height, features, 0)
+
+        def placed(x):
+            moved = jnp.where(first, pltpu.roll(x, order[0], 1), pltpu.roll(x, order[1], 1))
+            own = jnp.where(keep, moved, 0.0)
+            over = moved - own
+            return (own + half_swap(own))[0:channels], (over + half_swap(over))[0:channels]
+
+        def share(parts, own, own_in, spill, spill_in, at):
+            pairs = [placed(p) for p in parts]
+            spill[s] = joined_tiles([p[1] for p in pairs])
+            to_right = remote(spill.at[s], spill_in.at[s], edge_send.at[s, at], edge_recv.at[s, at], right)
+            to_right.start()
+            own[s] = joined_tiles([p[0] for p in pairs])
+            if last:
+                return [to_right]
+            to_left = remote(own.at[s], own_in.at[s], edge_send.at[s, at + 1], edge_recv.at[s, at + 1], left)
+            to_left.start()
+            return [to_right, to_left]
+
+        base = [
+            (next_a / now_a) * (window[h] - now_s * predicted[h]) + direction * predicted[h]
+            for h in range(height)
+        ]
+        edges = share(base, own_base, own_base_in, spill_base, spill_base_in, 0)
 
         await_all(anchor_buf.at[s], anchor_recv.at[s])
 
@@ -290,10 +369,9 @@
             stacked = taps[:, cols]
             total = None
             for i in range(per_dev):
-                d_joined = mm(wot[i], stacked).astype(BF16).astype(F32)
-                d_middle = (d_joined * deriv_m[i, :, cols]).astype(BF16)
-                d_act = mm(wmt[...], d_middle).astype(BF16).astype(F32)
-                d_hidden = (d_joined + d_act * deriv_h[i, :, cols]).astype(BF16)
+                d_joined = mm(wot[i], stacked).astype(BF16)
+                d_act = mm(wmt[...], d_joined * deriv_m[i, :, cols]).astype(BF16)
+                d_hidden = d_joined + d_act * deriv_h[i, :, cols]
                 piece = mm(wit[i], d_hidden)
                 total = piece if total is None else total + piece
             outward[:, cols] = total.astype(BF16).astype(F32)
@@ -311,33 +389,10 @@
         square_buf[s, 0] = square
         to_all(square_buf.at[s], square_send.at[s], square_recv.at[s])
 
-        def placed(x):
-            moved = jnp.where(first, pltpu.roll(x, starts[0], 1), pltpu.roll(x, starts[1], 1))
-            own = jnp.where(keep, moved, 0.0)
-            over = moved - own
-            return own + half_swap(own), over + half_swap(over)
-
-        own_parts, spill_parts = [], []
-        for h in range(height):
-            base = (next_a / now_a) * (window[h] - now_s * predicted[h]) + direction * predicted[h]
-            base_own, base_over = placed(base)
-            grad_own, grad_over = placed(gradient[h])
-            own_parts.append(jnp.where(first, base_own, grad_own))
-            spill_parts.append(jnp.where(first, base_over, grad_over))
-        spill_src[s] = joined_tiles(spill_parts)
-        to_right = remote(spill_src.at[s], spill_dst.at[s], edge_send.at[2 * s], edge_recv.at[2 * s], right)
-        to_right.start()
-        if not last:
-            own_src[s] = joined_tiles(own_parts)
-            to_left = remote(own_src.at[s], own_dst.at[s], edge_send.at[2 * s + 1], edge_recv.at[2 * s + 1], left)
-            to_left.start()
-
-        def merged(own, spill, coef, count, noise):
-            both = own + spill
-            swapped = half_swap(both)
-            base = jnp.where(first, both, swapped)
-            grad = jnp.where(first, swapped, both)
-            return (base - coef * grad) / count + spread * noise
+        edges += share(gradient, own_grad, own_grad_in, spill_grad, spill_grad_in, 2)
+
+        def merged(base, grad, coef, count, noise):
+            return (base - coef * grad) / all_tiles(count) + spread * noise
 
         await_all(square_buf.at[s], square_recv.at[s])
         square = square_buf[s, 0]
@@ -347,26 +402,24 @@
             1.0 / (n * rows * flat)
         )
         coef = (next_a / now_a) * guidance_ref[0] * lax.rsqrt(
-            jnp.broadcast_to(mean, (rows, width)) + STABILITY
-        )
-        to_right.wait()
-        spill = tiles(spill_dst[s])
+            jnp.broadcast_to(mean, (channels, flat)) + STABILITY
+        )
+        for edge in edges:
+            edge.wait()
+        block = merged(
+            own_base[s] + spill_base_in[s], own_grad[s] + spill_grad_in[s], coef, count_own,
+            0.0 if last else init_src[(s + 1) * channels : (s + 2) * channels, :],
+        )
         if last:
             for h in range(height):
-                noise = doubled(noise_ref[s, :, h, :])
-                out_ref[:, h, :] = merged(own_parts[h], spill[h], coef, count_own, noise)[0:channels, :]
+                out_ref[:, h, :] = block[:, h * width : (h + 1) * width] + spread * noise_ref[s, :, h, :]
         else:
-            to_left.wait()
-            noise_own = tiles(doubled(init_src[(s + 1) * channels : (s + 2) * channels, :]))
-            noise_next = tiles(doubled(init_dst[(s + 1) * channels : (s + 2) * channels, :]))
-            arrived = tiles(own_dst[s])
-            state = [
-                merged(own_parts[h], spill[h], coef, count_own, noise_own[h]) for h in range(height)
-            ]
-            state_next = [
-                merged(arrived[h], spill_parts[h], coef, count_next, noise_next[h])
-                for h in range(height)
-            ]
+            beyond = merged(
+                own_base_in[s] + spill_base[s], own_grad_in[s] + spill_grad[s], coef, count_next,
+                init_dst[(s + 1) * channels : (s + 2) * channels, :],
+            )
+            state = tiles(doubled(block))
+            state_next = tiles(doubled(beyond))
 
     for s in range(steps):
         await_all(anchor_buf.at[s], anchor_send.at[s])
@@ -384,25 +437,32 @@
     flat = height * width
     tall = len(TAP_SHIFTS) * rows
     vmem = pl.BlockSpec(memory_space=pltpu.VMEM)
-    smem = pl.BlockSpec(memory_space=pltpu.SMEM)
+    hbm = pl.BlockSpec(memory_space=pltpu.HBM)
+    operands = (latent, noise, offsets, anchors, guidance, w_in.T, w_mid, w_out, t_embed, w_feat.T)
+    in_smem = (2, 3, 4)
     dma = pltpu.SemaphoreType.DMA
     return pl.pallas_call(
         functools.partial(kernel, n, steps, per_dev, channels, height, width, hid, feat),
         out_shape=jax.ShapeDtypeStruct(latent.shape, F32),
-        in_specs=[vmem, vmem, smem, smem, smem, vmem, vmem, vmem, vmem, vmem],
+        in_specs=[hbm] * len(operands),
         out_specs=vmem,
         scratch_shapes=[
-            pltpu.VMEM((per_dev, hid, tall), BF16),
+            (pltpu.SMEM if k in in_smem else pltpu.VMEM)(x.shape, x.dtype)
+            for k, x in enumerate(operands)
+        ]
+        + [
+            dma((len(operands),)),
+            pltpu.VMEM((steps, per_dev, hid, tall + rows), BF16),
             pltpu.VMEM((per_dev, tall, hid), BF16),
             pltpu.VMEM((per_dev, tall, hid), BF16),
-            pltpu.VMEM((per_dev, hid, tall), BF16),
+            pltpu.VMEM((per_dev, hid, tall + rows), BF16),
             pltpu.VMEM((hid, hid), BF16),
-            pltpu.VMEM((steps, hid, WIN), F32),
+            pltpu.VMEM((hid, hid), BF16),
             pltpu.VMEM((channels, feat, width), F32),
-            pltpu.VMEM((tall, flat), BF16),
+            pltpu.VMEM((tall + rows, flat), BF16),
             pltpu.VMEM((tall, flat), F32),
-            pltpu.VMEM((per_dev, hid, flat), F32),
-            pltpu.VMEM((per_dev, hid, flat), F32),
+            pltpu.VMEM((per_dev, hid, flat), BF16),
+            pltpu.VMEM((per_dev, hid, flat), BF16),
             pltpu.VMEM((rows, flat), F32),
             pltpu.VMEM((per_dev, feat, flat), F32),
             pltpu.VMEM((per_dev, feat, flat), F32),
@@ -413,24 +473,21 @@
             pltpu.VMEM((2, rows, width), F32),
             pltpu.VMEM((steps, n, channels, flat), F32),
             pltpu.VMEM((steps, n, rows, width), F32),
-            pltpu.VMEM((steps, rows, flat), F32),
-            pltpu.VMEM((steps, rows, flat), F32),
-            pltpu.VMEM((steps, rows, flat), F32),
-            pltpu.VMEM((steps, rows, flat), F32),
+            *[pltpu.VMEM((steps, channels, flat), F32)] * 8,
             dma((3,)),
             dma((3,)),
             dma((steps,)),
             dma((steps,)),
             dma((steps,)),
             dma((steps,)),
-            dma((2 * steps,)),
-            dma((2 * steps,)),
+            dma((steps, 4)),
+            dma((steps, 4)),
         ],
         compiler_params=pltpu.CompilerParams(
-            collective_id=0, has_side_effects=True, vmem_limit_bytes=48 * 1024 * 1024
+            collective_id=0, has_side_effects=True, vmem_limit_bytes=67_000_000
         ),
         name="panorama",
-    )(latent, noise, offsets, anchors, guidance, w_in, w_mid, w_out, t_embed, w_feat)
+    )(*operands)
 
 
 def solution(mesh):

time: 47.6 us -> 43.3 us (0.910)
  Pallas kernels: 43.5 us -> 40.9 us
  local copies, waits for them, and re-layouts: 3.05 us -> 1.32 us
    pallas_call x1, Pallas kernels: 43.5 us -> 40.9 us  [local(): pl.pallas_call(functools.partial(kernel, n, steps, per_dev, channels, hei...]
    unnamed x19 -> x1, local copies, waits for them, and re-layouts: 3.05 us -> 1.32 us
where the time goes in v2:
time: 43.3 us; the launch traced here: 42.9 us
  Pallas kernels  40.9 us (94%)
  local copies, waits for them, and re-layouts  1.32 us (3%)
  between operations  0.66 us (2%)
    pallas_call x1, Pallas kernels, local(): pl.pallas_call(functools.partial(kernel, n, steps, per_dev, channels, hei...  40.9 us
    unnamed x1, local copies, waits for them, and re-layouts  1.32 us

profile of v2, /device:TPU:0, one launch (start us, length us, event | category | flops | bytes accessed | tf_op | source)
XLA Modules:
  0.0 42.9 jit_solution(11317991059043741059)
XLA Ops:
  0.7 40.9 %panorama.1 = f32[4,8,128]{2,1,0:T(8,128)} custom-call(f32[4,8,128]{2,1,0:T(8,128)} %latent_hbm.1, f32[2,4,8,128]{3,2,1,0:T(8,128)} %noise_hbm.1, s32[2]{0:T(128)} %offsets_hbm.1, s32[2]{0:T(128)} %anchors_hbm.1, f32[1]{0:T(128)S(6)} %copy.12.guidance_hbm, bf16[36,320]{1,0:T(8,128)(2,1)} %bitcast.2, bf16[320,320]{1,0:T(8,128)(2,1)} %w_mid_hbm.1, ...), custom_call_target="tpu_custom_call" | custom-call | tf_op jit(solution)/shard_map/panorama/pallas_call | solution.py:444
  41.6 1.3 %copy.13 = f32[4,8,128]{2,1,0:T(8,128)} copy(f32[4,8,128]{2,1,0:T(8,128)} %panorama.1) | data formatting | bytes 32768

commit v3 on v2

--- a/solution.py
+++ b/solution.py
@@ -10,8 +10,9 @@
 
 WIN = 128
 STRIDE = 64
-CHUNK = 256
-SIDE = 2
+CHUNK = 512
+SIDE = 1
+WIDE = 1024
 
 TAP_SHIFTS = ((-1, -1), (-1, 0), (-1, 1), (0, -1), (0, 0), (0, 1), (1, -1), (1, 0), (1, 1))
 CUMULATIVE_ALPHA = (0.35, 0.55, 0.72, 0.85, 0.93)
@@ -62,7 +63,7 @@
     latent_ref, noise_ref, offsets_ref, anchors_ref, guidance_ref,
     w_in_ref, w_mid_ref, w_out_ref, t_embed_ref, w_feat_ref, load_sem,
     wi, wit, wo, wot, wm, wmt, wfb,
-    taps, outward, deriv_h, deriv_m, clean_ref, per_a, per_d, dclean_ref,
+    taps, outward, second, deriv_h, deriv_m, clean_ref, per_a, per_d, dclean_ref,
     init_src, init_dst, cover_src, cover_dst,
     anchor_buf, square_buf, own_base, own_base_in, spill_base, spill_base_in,
     own_grad, own_grad_in, spill_grad, spill_grad_in,
@@ -279,7 +280,7 @@
         def forward(i):
             def block(j, carry):
                 for part in range(SIDE):
-                    cols = pl.ds(pl.multiple_of((j * SIDE + part) * CHUNK, CHUNK), CHUNK)
+                    cols = pl.ds(pl.multiple_of((j * SIDE + part) * WIDE, WIDE), WIDE)
                     stacked = taps[:, cols]
                     half, act, slope = silu_half(mm(wi[s, i], stacked))
                     act = act.astype(BF16)
@@ -287,11 +288,14 @@
                     act2, slope2 = silu_half(mm(wm[...], act))[1:]
                     deriv_m[i, :, cols] = slope2
                     piece = mm(wo[i], ((half + half) + act2).astype(BF16))
-                    outward[:, cols] = piece if i == 0 else outward[:, cols] + piece
+                    (outward if i == 0 else second)[:, cols] = piece
                 return carry
 
-            lax.fori_loop(0, flat // (CHUNK * SIDE), block, 0)
+            lax.fori_loop(0, flat // (WIDE * SIDE), block, 0)
             predicted = collapse(outward, 1)
+            if i == 1:
+                late = collapse(second, 1)
+                predicted = [jnp.where(first, p, q) for p, q in zip(predicted, late)]
             cleaned = [(window[h] - now_s * predicted[h]) * (1.0 / now_a) for h in range(height)]
             return predicted, cleaned
 
@@ -461,6 +465,7 @@
             pltpu.VMEM((channels, feat, width), F32),
             pltpu.VMEM((tall + rows, flat), BF16),
             pltpu.VMEM((tall, flat), F32),
+            pltpu.VMEM((tall, flat), F32),
             pltpu.VMEM((per_dev, hid, flat), BF16),
             pltpu.VMEM((per_dev, hid, flat), BF16),
             pltpu.VMEM((rows, flat), F32),

time: 43.3 us -> 39.1 us (0.903)
  Pallas kernels: 40.9 us -> 36.8 us
    pallas_call x1, Pallas kernels: 40.9 us -> 36.8 us  [local(): pl.pallas_call(functools.partial(kernel, n, steps, per_dev, channels, hei...]
where the time goes in v3:
time: 39.1 us; the launch traced here: 38.8 us
  Pallas kernels  36.8 us (94%)
  local copies, waits for them, and re-layouts  1.32 us (3%)
  between operations  0.66 us (2%)
    pallas_call x1, Pallas kernels, local(): pl.pallas_call(functools.partial(kernel, n, steps, per_dev, channels, hei...  36.8 us
    unnamed x1, local copies, waits for them, and re-layouts  1.32 us

profile of v3, /device:TPU:0, one launch (start us, length us, event | category | flops | bytes accessed | tf_op | source)
XLA Modules:
  0.0 38.8 jit_solution(16387075427093958632)
XLA Ops:
  0.7 36.8 %panorama.1 = f32[4,8,128]{2,1,0:T(8,128)} custom-call(f32[4,8,128]{2,1,0:T(8,128)} %latent_hbm.1, f32[2,4,8,128]{3,2,1,0:T(8,128)} %noise_hbm.1, s32[2]{0:T(128)} %offsets_hbm.1, s32[2]{0:T(128)} %anchors_hbm.1, f32[1]{0:T(128)S(6)} %copy.12.guidance_hbm, bf16[36,320]{1,0:T(8,128)(2,1)} %bitcast.2, bf16[320,320]{1,0:T(8,128)(2,1)} %w_mid_hbm.1, ...), custom_call_target="tpu_custom_call" | custom-call | tf_op jit(solution)/shard_map/panorama/pallas_call | solution.py:448
  37.5 1.3 %copy.13 = f32[4,8,128]{2,1,0:T(8,128)} copy(f32[4,8,128]{2,1,0:T(8,128)} %panorama.1) | data formatting | bytes 32768
